TPU v7x, 32 devices: a whole 2x2x4 slice. The times are simulated.
32 devices in a mesh: ga: 2 (over y), gx: 4 (over z), gy: 2 (over x), col: 2 (over core).
Axes of the slice: x: 2, y: 2, z: 4, core: 2. Of those that a mesh axis runs over, the one named last changes fastest.
Arguments:
- pair_rep: bfloat16 [2, 160, 160, 128], P('ga', 'gx', 'gy'), parts along dimension 0, may hold values from -6 to 6
- pair_mask: int32 [2, 160, 160], P('ga', 'gx', 'gy'), parts along dimension 0, may hold values 0 or 1
- amax_history: float32 [2, 128], P(None, 'col'), may hold values from 0.3 to 3
- in_gain: float32 [128], replicated, may hold values from 0.5 to 1.5
- in_bias: float32 [128], replicated, may hold values from -3 to 3
- proj_weight: bfloat16 [128, 4, 128], P(None, None, 'col'), may hold values from -0.5 to 0.5
- gate_weight: bfloat16 [128, 128], P(None, 'col'), may hold values from -0.5 to 0.5
- out_gain: float32 [128], replicated, may hold values from 0.5 to 1.5
- out_bias: float32 [128], replicated, may hold values from -3 to 3
- out_weight: bfloat16 [128, 128], P(None, 'col'), may hold values from -0.5 to 0.5
Outputs:
- update: bfloat16 [2, 160, 160, 128], P('ga', 'gx', 'gy', 'col'), parts along dimension 0
- new_amax: float32 [4, 128], P('ga', 'col'), parts along dimension 0
There are 2 independent parts, one for each index of `ga`. A program takes and returns all parts, laid end to end along the dimension named above; an argument that names none is the same for every part. Nothing has to cross between parts.
All inputs are finite; a program needn't handle non-finite values. No bound on the sum of `pair_mask` on one device may be relied on, other than what follows from the above.
Results may differ from a plain program's by a relative error of at most 0.0065.
Values may be sent and summed in bfloat16 or wider, within the bound.
A program may use at most 128 MiB of HBM per device.

v0:
```python
import jax
import jax.numpy as jnp
from jax import lax
from jax.sharding import PartitionSpec as P

epsilon = 1e-05
format_limit = 448.0


def broadcast(block, axis, holder):
    block = jnp.where(lax.axis_index(axis) == holder, block, jnp.zeros_like(block))
    return lax.psum(block, axis)


def layer_norm(values, gain, bias):
    average = jnp.mean(values, axis=-1, keepdims=True)
    spread = jnp.mean(jnp.square(values - average), axis=-1, keepdims=True)
    return (values - average) * lax.rsqrt(spread + epsilon) * gain + bias


def crop_triangle(left_q, right_q):
    wide_rows = lax.all_gather(right_q, "gy", axis=2, tiled=True)
    row_ratio = lax.axis_size("gx") // lax.axis_size("gy")
    first_root = lax.axis_index("gy") * row_ratio
    received = [
        broadcast(wide_rows, "gx", first_root + offset_step) for offset_step in range(row_ratio)
    ]
    panel = jnp.concatenate(received, axis=1)
    return jnp.einsum(
        "cik,cjk->cij",
        lax.all_gather(left_q, "gy", axis=2, tiled=True),
        panel,
        preferred_element_type=jnp.float32,
    )


def on_device(
    pair_rep,
    pair_mask,
    amax_history,
    in_gain,
    in_bias,
    proj_weight,
    gate_weight,
    out_gain,
    out_bias,
    out_weight,
):
    normed = layer_norm(pair_rep.astype(jnp.float32), in_gain, in_bias).astype(jnp.bfloat16)
    projected = jnp.einsum(
        "bikd,dsc->scbik", normed, proj_weight, preferred_element_type=jnp.float32
    )
    masking = pair_mask.astype(jnp.float32)[None]
    left_proj = masking * jax.nn.sigmoid(projected[1]) * projected[0]
    right_proj = masking * jax.nn.sigmoid(projected[3]) * projected[2]
    local_max = jnp.stack(
        [jnp.max(jnp.abs(left_proj), axis=(1, 2, 3)), jnp.max(jnp.abs(right_proj), axis=(1, 2, 3))]
    )
    new_amax = lax.pmax(local_max, ("gx", "gy"))
    scales = amax_history / format_limit
    left_q = jnp.clip(
        left_proj / scales[0][:, None, None, None], -format_limit, format_limit
    ).astype(jnp.bfloat16)
    right_q = jnp.clip(
        right_proj / scales[1][:, None, None, None], -format_limit, format_limit
    ).astype(jnp.bfloat16)
    products = jnp.stack([crop_triangle(left_q[:, 0], right_q[:, 0])], axis=1)
    triangle = (products * (scales[0] * scales[1])[:, None, None, None]).astype(jnp.bfloat16)
    gathered = lax.all_gather(triangle, "col", axis=0, tiled=True).astype(jnp.float32)
    average = jnp.mean(gathered, axis=0, keepdims=True)
    spread = jnp.mean(jnp.square(gathered - average), axis=0, keepdims=True)
    tnorm = (
        (gathered - average) * lax.rsqrt(spread + epsilon) * out_gain[:, None, None, None]
        + out_bias[:, None, None, None]
    ).astype(jnp.bfloat16)
    mixing = jnp.einsum("cbij,cd->bijd", tnorm, out_weight, preferred_element_type=jnp.float32)
    gating = jax.nn.sigmoid(
        jnp.einsum("bijd,dc->bijc", normed, gate_weight, preferred_element_type=jnp.float32)
    )
    update = (gating * mixing).astype(jnp.bfloat16)
    return (update, new_amax)


def solution(mesh):
    placed = (
        P("ga", "gx", "gy", None),
        P("ga", "gx", "gy"),
        P(None, "col"),
        P(),
        P(),
        P(None, None, "col"),
        P(None, "col"),
        P(),
        P(),
        P(None, "col"),
    )
    return jax.shard_map(
        on_device,
        mesh=mesh,
        in_specs=placed,
        out_specs=(P("ga", "gx", "gy", "col"), P("ga", "col")),
        check_vma=False,
    )
```

profile of v0, /device:TPU:3, one launch (start us, length us, event | category | flops | bytes accessed | tf_op | source)
XLA Modules:
  0.0 165.3 jit_solution(14759591514947378513)
XLA Ops:
  7.3 0.8 broadcast_multiply_fusion.2
  8.0 0.7 convert_bitcast_fusion.1
  8.8 1.6 convert_reduce_fusion.1
  10.4 1.2 fusion.13
  11.6 2.1 %convolution_bitcast_fusion = f32[4,64,40,80]{3,1,0,2:T(8,128)S(1)} fusion(bf16[1,40,80,128]{3,2,1,0:T(8,128)(2,1)S(1)} %copy-done.2, f32[128]{0:T(128)S(1)} %copy-done.6, f32[128]{0:T(128)S(1)} %copy-done.7, f32[40,80]{1,0:T(8,128)S(1)} %add_rsqrt_fusion.1, f32[40,80]{1,0:T(8,128)S(1)} %broadcast_multiply_fusion.1, bf16[128,4,64]{0,2,1:T(8,128)(2,1)S(1)} %copy-done), kind=kOutput, calls=%fused_computation.13 | convolution fusion | flops 212172800 | bytes 4188160 | tf_op jit(solution)/shard_map/bikd,dsc->scbik/dot_general | solution.py:50
  13.7 2.3 %fusion.45 = (bf16[64,40,80]{2,0,1:T(8,128)(2,1)S(1)}, bf16[64,40,80]{2,0,1:T(8,128)(2,1)}) fusion(f32[4,64,40,80]{3,1,0,2:T(8,128)S(1)} %convolution_bitcast_fusion, f32[64]{0:T(128)S(1)} %get-tuple-element.10, f32[40,80]{1,0:T(8,128)S(1)} %convert_bitcast_fusion.1, f32[64]{0:T(128)S(1)} %get-tuple-element.11), kind=kLoop, calls=%fused_computation.56 | loop fusion | flops 3276800 | bytes 4109312 | tf_op jit(solution)/shard_map/convert_element_type | solution.py:66
  16.3 0.5 copy.22
  16.7 19.8 %all_gather.10 = bf16[64,40,160]{0,1,2:T(8,128)(2,1)S(1)} all-gather(bf16[64,40,80]{0,1,2:T(8,128)(2,1)S(1)} %copy.22), channel_id=1, replica_groups=mesh['ga'=2,'gx'=4,'gy'=2,'col'=2] {'gy'}, dimensions={2}, use_global_device_ids=true | all-gather | bytes 1228800 | tf_op jit(solution)/shard_map/all_gather | solution.py:22
  36.5 4.0 %copy.23 = bf16[64,40,160]{2,1,0:T(8,128)(2,1)} copy(bf16[64,40,160]{0,1,2:T(8,128)(2,1)S(1)} %all_gather.10) | data formatting | bytes 1638400 | tf_op jit(solution)/shard_map/all_gather | solution.py:22
  40.5 3.0 %broadcast_select_fusion.1 = (bf16[64,40,160]{2,1,0:T(8,128)(2,1)}, bf16[64,40,160]{2,1,0:T(8,128)(2,1)}) fusion(bf16[64,40,160]{2,1,0:T(8,128)(2,1)} %copy.23, pred[]{:T(512)S(6)} %eq.6, pred[]{:T(512)S(6)} %eq.7), kind=kLoop, calls=%fused_computation.61 | loop fusion | flops 819200 | bytes 2457602 | tf_op jit(solution)/shard_map/jit(_where)/select_n | solution.py:11
  43.6 1.1 copy-done.3
  44.7 0.5 copy.20
  45.1 19.0 %all_gather.9 = bf16[64,40,160]{0,1,2:T(8,128)(2,1)S(1)} all-gather(bf16[64,40,80]{0,1,2:T(8,128)(2,1)S(1)} %copy.20), channel_id=1, replica_groups=mesh['ga'=2,'gx'=4,'gy'=2,'col'=2] {'gy'}, dimensions={2}, use_global_device_ids=true | all-gather | bytes 1228800 | tf_op jit(solution)/shard_map/all_gather | solution.py:31
  64.2 4.0 %copy.25 = bf16[64,40,160]{2,1,0:T(8,128)(2,1)} copy(bf16[64,40,160]{0,1,2:T(8,128)(2,1)S(1)} %all_gather.9) | data formatting | bytes 1638400 | tf_op jit(solution)/shard_map/all_gather | solution.py:31
  68.2 3.5 %fusion.37 = (f32[64]{0:T(128)S(1)}, f32[64]{0:T(128)S(1)}) fusion(f32[4,64,40,80]{3,1,0,2:T(8,128)} %copy-done.1, f32[40,80]{1,0:T(8,128)S(1)} %convert_bitcast_fusion.1), kind=kLoop, calls=%fused_computation.43 | loop fusion | flops 2867072 | bytes 3290112 | tf_op jit(solution)/shard_map/reduce_max | solution.py:57
  71.7 16.0 %pmax.7 = f32[2,64]{1,0:T(2,128)} all-reduce(f32[2,64]{1,0:T(2,128)S(1)} %pad_maximum_fusion), channel_id=1, replica_groups=mesh['ga'=2,'gx'=4,'gy'=2,'col'=2] {'gx','gy'}, use_global_device_ids=true, to_apply=%region_8.9 | all-reduce | flops 128 | bytes 1024 | tf_op jit(solution)/shard_map/pmax | solution.py:59
  87.7 0.5 fusion.58
  88.2 2.0 %fusion.22 = f32[40,80,64]{1,2,0:T(8,128)S(1)} fusion(bf16[1,40,80,128]{3,2,1,0:T(8,128)(2,1)S(1)} %copy-done.2, f32[128]{0:T(128)S(1)} %copy-done.6, f32[128]{0:T(128)S(1)} %copy-done.7, f32[40,80]{1,0:T(8,128)S(1)} %add_rsqrt_fusion.1, f32[40,80]{1,0:T(8,128)S(1)} %broadcast_multiply_fusion.1, bf16[128,64]{0,1:T(8,128)(2,1)} %param.16), kind=kOutput, calls=%fused_computation.27 | convolution fusion | flops 55500800 | bytes 1681408 | tf_op jit(solution)/shard_map/bijd,dc->bijc/dot_general | solution.py:78
  90.2 59.8 %all-reduce.3.cloned.1.call-done = (bf16[64,40,160]{2,1,0:T(8,128)(2,1)}, bf16[64,40,160]{2,1,0:T(8,128)(2,1)}) async-done(((bf16[64,40,160]{2,1,0:T(8,128)(2,1)}, bf16[64,40,160]{2,1,0:T(8,128)(2,1)}), (bf16[64,40,160]{2,1,0:T(8,128)(2,1)}, bf16[64,40,160]{2,1,0:T(8,128)(2,1)})) %all-reduce.3.cloned.1.call-update) | async-done | bytes 1638416 | tf_op jit(solution)/shard_map/psum | solution.py:12
  150.0 2.5 %fusion.24 = bf16[64,40,80]{2,1,0:T(8,128)(2,1)S(1)} fusion(bf16[64,40,160]{2,1,0:T(8,128)(2,1)S(1)} %copy-done.4, bf16[64,40,160]{2,1,0:T(8,128)(2,1)} %get-tuple-element.4, bf16[64,40,160]{2,1,0:T(8,128)(2,1)} %get-tuple-element.5, f32[64]{0:T(128)} %fusion.58), kind=kOutput, calls=%fused_computation.29 | convolution fusion | flops 69222400 | bytes 2867456 | tf_op jit(solution)/shard_map/cik,cjk->cij/dot_general | solution.py:29
  152.6 3.2 %all-gather = bf16[128,40,80]{2,1,0:T(8,128)(2,1)S(1)} all-gather(bf16[64,40,80]{2,1,0:T(8,128)(2,1)S(1)} %fusion.24), channel_id=2, replica_groups=mesh['ga'=2,'gx'=4,'gy'=2,'col'=2] {'col'}, dimensions={0}, use_global_device_ids=true | all-gather | bytes 1228800 | tf_op jit(solution)/shard_map/all_gather | solution.py:69
  156.1 0.5 fusion.3
  156.6 0.5 fusion.27
  157.3 1.2 fusion.47
  (28 shorter events, 0.8 us)
Async XLA Ops:
  7.2 4.4 %copy-start = (bf16[128,4,64]{0,2,1:T(8,128)(2,1)S(1)}, bf16[128,4,64]{0,2,1:T(8,128)(2,1)}, u32[]{:S(2)}) copy-start(bf16[128,4,64]{0,2,1:T(8,128)(2,1)} %param.15) | copy-start | bytes 196612
  7.2 3.2 %copy-start.2 = (bf16[1,40,80,128]{3,2,1,0:T(8,128)(2,1)S(1)}, bf16[1,40,80,128]{3,2,1,0:T(8,128)(2,1)}, u32[]{:S(2)}) copy-start(bf16[1,40,80,128]{3,2,1,0:T(8,128)(2,1)} %param.10) | copy-start | bytes 2457604
  7.2 4.4 %copy-start.6 = (f32[128]{0:T(128)S(1)}, f32[128]{0:T(128)}, u32[]{:S(2)}) copy-start(f32[128]{0:T(128)} %param.14) | copy-start | bytes 1540
  7.2 4.4 %copy-start.7 = (f32[128]{0:T(128)S(1)}, f32[128]{0:T(128)}, u32[]{:S(2)}) copy-start(f32[128]{0:T(128)} %param.13) | copy-start | bytes 1540
  7.2 142.8 %all-reduce.3.cloned.1.call-start = ((), (), s32[]{:S(2)}) async-start(), calls=%async_computation | async-start | bytes 5242880 | tf_op jit(solution)/shard_map/psum | solution.py:12
  13.7 2.5 %copy-start.1 = (f32[4,64,40,80]{3,1,0,2:T(8,128)}, f32[4,64,40,80]{3,1,0,2:T(8,128)S(1)}, u32[]{:S(2)}) copy-start(f32[4,64,40,80]{3,1,0,2:T(8,128)S(1)} %convolution_bitcast_fusion) | copy-start | bytes 9830404
  43.6 1.1 copy-start.3
  88.2 61.8 %copy-start.4 = (bf16[64,40,160]{2,1,0:T(8,128)(2,1)S(1)}, bf16[64,40,160]{2,1,0:T(8,128)(2,1)}, u32[]{:S(2)}) copy-start(bf16[64,40,160]{2,1,0:T(8,128)(2,1)} %copy.25) | copy-start | bytes 2457604
  155.8 0.8 copy-start.8
  155.8 0.8 copy-start.9
  156.6 0.7 copy-start.5
Sparse Core Ops, SparseCore 0:
  43.7 106.2 all-reduce.2
where the time goes:
time: 167 us; the launch traced here: 165 us
  waiting for transfers between devices  59.9 us (36%)
  blocking collectives  58 us (35%)
  other arithmetic  15 us (9%)
  between operations  14.2 us (9%)
  local copies, waits for them, and re-layouts  10.5 us (6%)
  matrix products  7.78 us (5%)
    psum x1, waiting for transfers between devices, broadcast(): return lax.psum(block, axis)  59.8 us
    all_gather x1, blocking collectives, crop_triangle(): wide_rows = lax.all_gather(right_q, 'gy', axis=2, tiled=True)  19.8 us
    all_gather x1, blocking collectives, crop_triangle(): lax.all_gather(left_q, 'gy', axis=2, tiled=True)  19 us
    pmax x1, blocking collectives, on_device(): new_amax = lax.pmax(local_max, ('gx', 'gy'))  16 us
    all_gather x1, local copies, waits for them, and re-layouts, crop_triangle(): lax.all_gather(left_q, 'gy', axis=2, tiled=True)  4.05 us
    all_gather x1, local copies, waits for them, and re-layouts, crop_triangle(): wide_rows = lax.all_gather(right_q, 'gy', axis=2, tiled=True)  4.02 us
    reduce_max x1, other arithmetic, on_device(): jnp.max(jnp.abs(left_proj), axis=(1, 2, 3))  3.51 us
  transfers between devices with their start and end apart: 1, of which 1 were waited for; matrix products, arithmetic and copies ran while one was open for 6% of the time, Pallas kernels for 0%

commit v1 on v0

v1 whole, which is shorter than its diff:
```python
import functools

import jax
import jax.numpy as jnp
from jax import lax
from jax.experimental import pallas as pl
from jax.experimental.pallas import tpu as pltpu
from jax.sharding import PartitionSpec as P

epsilon = 1e-05
format_limit = 448.0
LANES = 128
f32, bf16 = jnp.float32, jnp.bfloat16
MESH = pl.DeviceIdType.MESH


def kernel(
    dims,
    rep_ref,
    mask_ref,
    hist_ref,
    hist_smem,
    in_gain_ref,
    in_bias_ref,
    proj_ref,
    gate_ref,
    out_gain_smem,
    out_bias_smem,
    out_weight_ref,
    out_ref,
    amax_ref,
    normed,
    maskf,
    inverse,
    peak,
    left_s,
    right_s,
    left_b,
    right_all,
    own_t,
    send_t,
    recv_t,
    full_t,
    spread_t,
    mix_w,
    ow_pad,
    gating,
    peaks,
    peak_send,
    peak_recv,
    z_send,
    z_recv,
    x_send,
    x_recv,
    c_send,
    c_recv,
):
    nz, ny, rows, cols, half, chunks = dims
    ratio = nz // ny
    channels = 2 * half
    per = LANES // rows
    pairs = -(-half // (2 * per))
    groups = 2 * pairs
    span = per * rows
    slot = LANES // (2 * ratio)
    z, y, col = lax.axis_index("gx"), lax.axis_index("gy"), lax.axis_index("col")
    members = nz * ny
    me = z * ny + y

    barrier = pltpu.get_barrier_semaphore()

    def greet(t, carry):
        peer = lax.rem(me + t, members)
        pl.semaphore_signal(
            barrier, inc=1, device_id={"gx": peer // ny, "gy": lax.rem(peer, ny)}, device_id_type=MESH
        )
        return carry

    lax.fori_loop(1, members, greet, 0)
    pl.semaphore_signal(barrier, inc=1, device_id={"col": 1 - col}, device_id_type=MESH)

    normed[pl.ds(rows * cols, LANES), :] = jnp.zeros((LANES, channels), bf16)
    step_rows = 4

    def norm_step(b, carry):
        values = rep_ref[pl.ds(b * step_rows, step_rows)].reshape(step_rows * cols, channels).astype(f32)
        average = jnp.mean(values, axis=-1, keepdims=True)
        centred = values - average
        var = jnp.mean(jnp.square(centred), axis=-1, keepdims=True)
        result = centred * lax.rsqrt(var + epsilon) * in_gain_ref[...] + in_bias_ref[...]
        start = pl.multiple_of(b * step_rows * cols, 16)
        normed[pl.ds(start, step_rows * cols), :] = result.astype(bf16)
        return carry

    lax.fori_loop(0, rows // step_rows, norm_step, 0)
    maskf[...] = jnp.zeros_like(maskf)
    maskf[:, 0:cols] = mask_ref[...].astype(f32)
    flipped = jnp.broadcast_to(format_limit / hist_ref[...], (channels, channels))
    inverse[...] = jnp.transpose(flipped)
    peak[...] = jnp.zeros_like(peak)
    tail = left_s.shape[0] - half * rows
    left_s[pl.ds(half * rows, tail), :] = jnp.zeros((tail, LANES), f32)
    right_s[pl.ds(half * rows, tail), :] = jnp.zeros((tail, LANES), f32)

    def project(side, target):
        base = side * half

        def one(i):
            block = normed[pl.ds(pl.multiple_of(i * cols, 16), LANES), :]
            p = lax.dot_general(
                proj_ref[2 * base : 2 * base + channels, :],
                block,
                (((1,), (1,)), ((), ())),
                preferred_element_type=f32,
            )
            value = jax.nn.sigmoid(p[half:]) * p[:half] * maskf[pl.ds(i, 1), :]
            target[pl.ds(i, half, stride=rows), :] = jnp.clip(
                value * inverse[base : base + half, :], -format_limit, format_limit
            )
            return jnp.abs(value)

        def step(b, top):
            for u in range(4):
                top = jnp.maximum(top, one(b * 4 + u))
            return top

        top = lax.fori_loop(0, rows // 4, step, jnp.zeros((half, LANES), f32))
        peak[base : base + half, :] = top

    project(1, right_s)
    bounds = [pairs * c // chunks for c in range(chunks + 1)]

    def z_copy(source, c, direction):
        window = pl.ds(2 * bounds[c], 2 * (bounds[c + 1] - bounds[c]))
        toward = z + 1 if direction == 0 else z - 1
        return pltpu.make_async_remote_copy(
            src_ref=right_all.at[source, window],
            dst_ref=right_all.at[source, window],
            send_sem=z_send.at[direction, source, c],
            recv_sem=z_recv.at[source, c],
            device_id={"gx": toward},
            device_id_type=MESH,
        )

    pl.semaphore_wait(barrier, members)
    for c in range(chunks):
        for g in range(2 * bounds[c], 2 * bounds[c + 1]):
            tile = jnp.transpose(right_s[g * span : g * span + LANES, :])
            right_all[z, g] = tile[:cols].astype(bf16)

        @pl.when(z < nz - 1)
        def _():
            z_copy(z, c, 0).start()

        @pl.when(z > 0)
        def _():
            z_copy(z, c, 1).start()

    project(0, left_s)
    for g in range(groups):
        left_b[g] = left_s[g * span : g * span + LANES, :].astype(bf16)

    peaks[me] = jnp.broadcast_to(jnp.max(jnp.transpose(peak[...]), axis=0, keepdims=True), (8, channels))

    def spread_peak(t, carry):
        peer = lax.rem(me + t, members)
        pltpu.make_async_remote_copy(
            src_ref=peaks.at[me],
            dst_ref=peaks.at[me],
            send_sem=peak_send,
            recv_sem=peak_recv,
            device_id={"gx": peer // ny, "gy": lax.rem(peer, ny)},
            device_id_type=MESH,
        ).start()
        return carry

    lax.fori_loop(1, members, spread_peak, 0)

    lane = lax.broadcasted_iota(jnp.int32, (rows, LANES), 1)

    def triangle_pair(r, p):
        halves = []
        for u in range(2):
            res = lax.dot_general(
                left_b[2 * p + u][:, :cols],
                right_all[r, 2 * p + u],
                (((1,), (0,)), ((), ())),
                preferred_element_type=f32,
            )
            t = res[:rows]
            for s in range(1, per):
                t = jnp.where(lane >= s * rows, res[s * rows : (s + 1) * rows], t)
            halves.append(t)
        return jnp.concatenate(halves, axis=0)

    def x_copy(target, sub, c, source):
        window = pl.ds(bounds[c], bounds[c + 1] - bounds[c])
        return pltpu.make_async_remote_copy(
            src_ref=send_t.at[target, sub, window],
            dst_ref=recv_t.at[source, sub, window],
            send_sem=x_send.at[target, sub, c],
            recv_sem=x_recv.at[source, sub, c],
            device_id={"gy": target},
            device_id_type=MESH,
        )

    def triangle_block(r, c):
        owner, sub = r // ratio, lax.rem(r, ratio)

        @pl.when(owner == y)
        def _():
            for p in range(bounds[c], bounds[c + 1]):
                own_t[sub, p] = triangle_pair(r, p)

        @pl.when(owner != y)
        def _():
            for p in range(bounds[c], bounds[c + 1]):
                send_t[owner, sub, p] = triangle_pair(r, p).astype(bf16)
            x_copy(owner, sub, c, y).start()

    def own_block(c):
        triangle_block(z, c)

    for c in range(chunks):
        own_block(c)

    def gate_step(b, carry):
        size = step_rows * cols
        start = pl.multiple_of(b * size, 16)
        gating[pl.ds(start, size), :] = jax.nn.sigmoid(
            jnp.dot(normed[pl.ds(start, size), :], gate_ref[...], preferred_element_type=f32)
        )
        return carry

    lax.fori_loop(0, rows // step_rows, gate_step, 0)
    ow_pad[...] = jnp.zeros_like(ow_pad)
    stretch = ow_pad.shape[0] // 2
    for cc in range(2):
        ow_pad[cc * stretch : cc * stretch + half, 0:half] = out_weight_ref[
            cc * half : (cc + 1) * half, :
        ].astype(f32)
    mix_w[...] = jnp.zeros_like(mix_w)
    for rr in range(ratio):
        for s in range(per):
            for cc in range(2):
                piece = ow_pad[pl.ds(cc * stretch + s, slot, stride=per), :]
                at = rr * 2 * slot + cc * slot
                mix_w[rr, s, at : at + slot, :] = piece.astype(bf16)
    spread_t[...] = jnp.zeros_like(spread_t)

    def ring_step(d, carry):
        low, high = z - d, z + d
        for c in range(chunks):

            @pl.when(low >= 0)
            def _():
                z_copy(low, c, 0).wait_recv()

                @pl.when(z < nz - 1)
                def _():
                    z_copy(low, c, 0).start()

            @pl.when(high < nz)
            def _():
                z_copy(high, c, 1).wait_recv()

                @pl.when(z > 0)
                def _():
                    z_copy(high, c, 1).start()

            @pl.when(low >= 0)
            def _():
                triangle_block(low, c)

            @pl.when(high < nz)
            def _():
                triangle_block(high, c)

        return carry

    lax.fori_loop(1, nz, ring_step, 0)

    group_lane = lax.broadcasted_iota(jnp.int32, (1, LANES), 1)

    def lane_vector(scalar_of):
        vector = jnp.full((1, LANES), scalar_of(0), f32)
        for s in range(1, per):
            vector = jnp.where(group_lane >= s * rows, scalar_of(s), vector)
        return vector

    def pair_vector(scalar_of, p):
        parts = []
        for u in range(2):
            g = 2 * p + u
            vector = lane_vector(lambda s: scalar_of(g * per + s))
            parts.append(jnp.broadcast_to(vector, (rows, LANES)))
        return jnp.concatenate(parts, axis=0)

    def scale_of(ch):
        ch = jnp.minimum(ch, half - 1)
        return (hist_smem[0, ch] / format_limit) * (hist_smem[1, ch] / format_limit)

    def c_copy(sub, c):
        window = pl.ds(bounds[c], bounds[c + 1] - bounds[c])
        return pltpu.make_async_remote_copy(
            src_ref=full_t.at[col, sub, window],
            dst_ref=full_t.at[col, sub, window],
            send_sem=c_send.at[sub, c],
            recv_sem=c_recv.at[sub, c],
            device_id={"col": 1 - col},
            device_id_type=MESH,
        )

    for sub in range(ratio):
        for c in range(chunks):

            def arrive(t, carry):
                x_copy(y, sub, c, lax.rem(y + t, ny)).wait_recv()
                return carry

            lax.fori_loop(1, ny, arrive, 0)

            def finish(p, carry):
                total = own_t[sub, p]
                for t in range(1, ny):
                    total = total + recv_t[lax.rem(y + t, ny), sub, p].astype(f32)
                full_t[col, sub, p] = (total * pair_vector(scale_of, p)).astype(bf16)
                return carry

            lax.fori_loop(bounds[c], bounds[c + 1], finish, 0)
            c_copy(sub, c).start()

    valid = lax.broadcasted_iota(jnp.int32, (2 * rows, LANES), 1) < 0
    row_at = lax.broadcasted_iota(jnp.int32, (2 * rows, LANES), 0) // rows
    lane_at = lax.broadcasted_iota(jnp.int32, (2 * rows, LANES), 1) // rows
    valid = (((pairs - 1) * 2 + row_at) * per + lane_at) < half

    def segment_mean(pair_sum):
        x = pair_sum[:rows] + pair_sum[rows:]
        total = x
        for s in range(1, per):
            total = total + pltpu.roll(x, s * rows, 1)
        result = total
        for s in range(1, per):
            moved = pltpu.roll(total, LANES - s * rows, 1)
            result = jnp.where(lane < (per - s) * rows, moved, result)
        result = result * (1.0 / channels)
        return jnp.concatenate([result, result], axis=0)

    for sub in range(ratio):
        for c in range(chunks):
            c_copy(sub, c).wait_recv()

        def add_up(p, total):
            return total + full_t[0, sub, p].astype(f32) + full_t[1, sub, p].astype(f32)

        zero = jnp.zeros((2 * rows, LANES), f32)
        mean = segment_mean(lax.fori_loop(0, pairs, add_up, zero))

        def add_squares(p, total):
            for cc in range(2):
                total = total + jnp.square(full_t[cc, sub, p].astype(f32) - mean)
            return total

        squares = lax.fori_loop(0, pairs - 1, add_squares, zero)
        for cc in range(2):
            last = jnp.square(full_t[cc, sub, pairs - 1].astype(f32) - mean)
            squares = squares + jnp.where(valid, last, 0.0)
        factor = lax.rsqrt(segment_mean(squares) + epsilon)

        def normalise(p, carry):
            for cc in range(2):

                def gain_of(ch, cc=cc):
                    return out_gain_smem[cc * half + jnp.minimum(ch, half - 1)]

                def bias_of(ch, cc=cc):
                    return out_bias_smem[cc * half + jnp.minimum(ch, half - 1)]

                t = (full_t[cc, sub, p].astype(f32) - mean) * factor
                t = t * pair_vector(gain_of, p) + pair_vector(bias_of, p)
                for u in range(2):
                    at = (sub * 2 + cc) * slot + 2 * p + u
                    spread_t[pl.ds(at, rows, stride=LANES), :] = t[u * rows : (u + 1) * rows]
            return carry

        lax.fori_loop(0, pairs, normalise, 0)

    batch = 8

    def mix_step(b, carry):
        pieces = [[] for _ in range(per)]
        for u in range(batch):
            start = pl.multiple_of((b * batch + u) * LANES, LANES)
            tile = jnp.transpose(spread_t[pl.ds(start, LANES), :])
            for s in range(per):
                pieces[s].append(tile[s * rows : (s + 1) * rows])
        blocks = [jnp.concatenate(piece, axis=0).astype(bf16) for piece in pieces]
        mixed = []
        for rr in range(ratio):
            total = jnp.dot(blocks[0], mix_w[rr, 0], preferred_element_type=f32)
            for s in range(1, per):
                total = total + jnp.dot(blocks[s], mix_w[rr, s], preferred_element_type=f32)
            mixed.append(total[:, :half].reshape(batch, rows, half))
        mixing = jnp.concatenate(mixed, axis=1)
        start = pl.multiple_of(b * batch * cols, 16)
        gates = gating[pl.ds(start, batch * cols), :].reshape(batch, cols, half)
        out_ref[pl.ds(b * batch, batch)] = (gates * mixing).astype(bf16)
        return carry

    lax.fori_loop(0, rows // batch, mix_step, 0)

    others = peaks.at[pl.ds(0, members - 1)]
    pltpu.make_async_copy(others, others, peak_recv).wait()
    top = jnp.max(jnp.max(peaks[...], axis=0), axis=0, keepdims=True)
    amax_ref[0:1, :] = top[:, :half]
    amax_ref[1:2, :] = top[:, half:]

    pltpu.make_async_copy(others, others, peak_send).wait()
    for sub in range(ratio):
        for c in range(chunks):
            c_copy(sub, c).wait_send()

    def drain_x(t, carry):
        for sub in range(ratio):
            for c in range(chunks):
                x_copy(lax.rem(y + t, ny), sub, c, y).wait_send()
        return carry

    lax.fori_loop(1, ny, drain_x, 0)

    def drain_z(source, carry):
        for c in range(chunks):

            @pl.when((source <= z) & (z < nz - 1))
            def _():
                z_copy(source, c, 0).wait_send()

            @pl.when((source >= z) & (z > 0))
            def _():
                z_copy(source, c, 1).wait_send()

        return carry

    lax.fori_loop(0, nz, drain_z, 0)


def on_device(
    nz,
    ny,
    pair_rep,
    pair_mask,
    amax_history,
    in_gain,
    in_bias,
    proj_weight,
    gate_weight,
    out_gain,
    out_bias,
    out_weight,
):
    crops, rows, cols, channels = pair_rep.shape
    half = proj_weight.shape[2]
    chunks = 2
    ratio = nz // ny
    per = LANES // rows
    pairs = -(-half // (2 * per))
    groups = 2 * pairs
    slot = LANES // (2 * ratio)
    members = nz * ny
    weights = jnp.transpose(proj_weight, (1, 2, 0)).reshape(4 * half, channels)
    scratch_rows = -(-((groups - 1) * per * rows + LANES) // 8) * 8
    dma = pltpu.SemaphoreType.DMA
    vmem = pl.BlockSpec(memory_space=pltpu.VMEM)
    smem = pl.BlockSpec(memory_space=pltpu.SMEM)
    tile = (2 * rows, LANES)
    update, new_amax = pl.pallas_call(
        functools.partial(kernel, (nz, ny, rows, cols, half, chunks)),
        out_shape=(
            jax.ShapeDtypeStruct((rows, cols, half), bf16),
            jax.ShapeDtypeStruct((2, half), f32),
        ),
        in_specs=[vmem, vmem, vmem, smem, vmem, vmem, vmem, vmem, smem, smem, vmem],
        out_specs=(vmem, vmem),
        scratch_shapes=[
            pltpu.VMEM((rows * cols + LANES, channels), bf16),
            pltpu.VMEM((rows, LANES), f32),
            pltpu.VMEM((channels, LANES), f32),
            pltpu.VMEM((channels, LANES), f32),
            pltpu.VMEM((scratch_rows, LANES), f32),
            pltpu.VMEM((scratch_rows, LANES), f32),
            pltpu.VMEM((groups, LANES, LANES), bf16),
            pltpu.VMEM((nz, groups, cols, LANES), bf16),
            pltpu.VMEM((ratio, pairs) + tile, f32),
            pltpu.VMEM((ny, ratio, pairs) + tile, bf16),
            pltpu.VMEM((ny, ratio, pairs) + tile, bf16),
            pltpu.VMEM((2, ratio, pairs) + tile, bf16),
            pltpu.VMEM((rows * LANES, LANES), f32),
            pltpu.VMEM((ratio, per, LANES, LANES), bf16),
            pltpu.VMEM((2 * slot * per, LANES), f32),
            pltpu.VMEM((rows * cols, half), f32),
            pltpu.VMEM((members, 8, channels), f32),
            dma,
            dma,
            dma((2, nz, chunks)),
            dma((nz, chunks)),
            dma((ny, ratio, chunks)),
            dma((ny, ratio, chunks)),
            dma((ratio, chunks)),
            dma((ratio, chunks)),
        ],
        compiler_params=pltpu.CompilerParams(
            collective_id=0, has_side_effects=True, vmem_limit_bytes=56 * 1024 * 1024
        ),
    )(
        pair_rep[0],
        pair_mask[0],
        amax_history.reshape(1, channels),
        amax_history,
        in_gain.reshape(1, channels),
        in_bias.reshape(1, channels),
        weights,
        gate_weight,
        out_gain,
        out_bias,
        out_weight,
    )
    return update[None], new_amax


def solution(mesh):
    placed = (
        P("ga", "gx", "gy", None),
        P("ga", "gx", "gy"),
        P(None, "col"),
        P(),
        P(),
        P(None, None, "col"),
        P(None, "col"),
        P(),
        P(),
        P(None, "col"),
    )
    return jax.shard_map(
        functools.partial(on_device, mesh.shape["gx"], mesh.shape["gy"]),
        mesh=mesh,
        in_specs=placed,
        out_specs=(P("ga", "gx", "gy", "col"), P("ga", "col")),
        check_vma=False,
    )
```

time: 167 us -> 56.6 us (0.34)
  the two profiles are of different devices: /device:TPU:3 before, /device:TPU:25 now
where the time goes in v1:
time: 56.6 us; the launch traced here: 56.3 us
  Pallas kernels  49.4 us (87%)
  local copies, waits for them, and re-layouts  6.25 us (11%)
  between operations  0.66 us (1%)
    pallas_call x1, Pallas kernels, on_device(): pl.pallas_call(functools.partial(kernel, (nz, ny, rows, cols, half, chunk...  49.4 us
    unnamed x10, local copies, waits for them, and re-layouts  5.66 us

profile of v1, /device:TPU:25, one launch (start us, length us, event | category | flops | bytes accessed | tf_op | source)
XLA Modules:
  0.0 56.3 jit_solution(4991871698809700279)
XLA Ops:
  0.6 0.0 copy-start.2
  0.6 0.7 %copy-done.2 = f32[2,64]{1,0:T(2,128)S(1)} copy-done((f32[2,64]{1,0:T(2,128)S(1)}, f32[2,64]{1,0:T(2,128)}, u32[]{:S(2)}) %copy-start.2) | copy-done | bytes 536
  1.3 0.6 %reshape.16.hist_ref = f32[1,128]{1,0:T(1,128)} reshape(f32[2,64]{1,0:T(2,128)S(1)} %copy-done.2) | data formatting | bytes 1024 | tf_op jit(solution)/shard_map/reshape | solution.py:518
  1.9 0.0 copy-start
  1.9 1.4 %copy.12.gate_ref = bf16[128,64]{1,0:T(8,128)(2,1)} copy(bf16[128,64]{0,1:T(8,128)(2,1)} %param.16) | data formatting | bytes 32768 | tf_op args[6]
  3.4 0.0 copy-done
  3.4 0.7 %copy.13.out_weight_ref = bf16[128,64]{1,0:T(8,128)(2,1)} copy(bf16[128,64]{0,1:T(8,128)(2,1)S(1)} %copy-done) | data formatting | bytes 32768 | tf_op args[9]
  4.1 49.4 %shard_map.113 = (bf16[40,80,64]{2,1,0:T(8,128)(2,1)}, f32[2,64]{1,0:T(2,128)}) custom-call(bf16[40,80,128]{2,1,0:T(8,128)(2,1)} %bitcast.8, s32[40,80]{1,0:T(8,128)} %bitcast.11, f32[1,128]{1,0:T(1,128)} %reshape.16.hist_ref, f32[2,64]{1,0:T(2,128)} %hist_smem.1, f32[1,128]{1,0:T(1,128)} %bitcast.12, f32[1,128]{1,0:T(1,128)} %bitcast.13, ...), custom_call_target="tpu_custom_call" | custom-call | tf_op jit(solution)/shard_map/pallas_call | solution.py:477
  53.5 0.0 copy-start.1
  53.5 2.3 %copy.14 = bf16[1,40,80,64]{2,3,1,0:T(8,128)(2,1)} copy(bf16[1,40,80,64]{3,2,1,0:T(8,128)(2,1)} %bitcast.9) | data formatting | bytes 819200
  55.8 0.0 copy-done.1
  55.8 0.6 copy.16
Async XLA Ops:
  0.6 0.7 %copy-start.2 = (f32[2,64]{1,0:T(2,128)S(1)}, f32[2,64]{1,0:T(2,128)}, u32[]{:S(2)}) copy-start(f32[2,64]{1,0:T(2,128)} %hist_smem.1) | copy-start | bytes 1540
  1.9 1.5 %copy-start = (bf16[128,64]{0,1:T(8,128)(2,1)S(1)}, bf16[128,64]{0,1:T(8,128)(2,1)}, u32[]{:S(2)}) copy-start(bf16[128,64]{0,1:T(8,128)(2,1)} %param.19) | copy-start | bytes 49156
  53.5 2.3 %copy-start.1 = (f32[2,64]{1,0:T(2,128)S(1)}, f32[2,64]{1,0:T(2,128)}, u32[]{:S(2)}) copy-start(f32[2,64]{1,0:T(2,128)} %get-tuple-element.11) | copy-start | bytes 1540

commit v2 on v1

--- a/solution.py
+++ b/solution.py
@@ -95,7 +95,9 @@
     lax.fori_loop(0, rows // step_rows, norm_step, 0)
     maskf[...] = jnp.zeros_like(maskf)
     maskf[:, 0:cols] = mask_ref[...].astype(f32)
-    flipped = jnp.broadcast_to(format_limit / hist_ref[...], (channels, channels))
+    scaled = format_limit / hist_ref[...]
+    flipped = jnp.concatenate([scaled[0:1], scaled[1:2]], axis=1)
+    flipped = jnp.broadcast_to(flipped, (channels, channels))
     inverse[...] = jnp.transpose(flipped)
     peak[...] = jnp.zeros_like(peak)
     tail = left_s.shape[0] - half * rows
@@ -225,27 +227,30 @@
         own_block(c)
 
     def gate_step(b, carry):
-        size = step_rows * cols
-        start = pl.multiple_of(b * size, 16)
-        gating[pl.ds(start, size), :] = jax.nn.sigmoid(
-            jnp.dot(normed[pl.ds(start, size), :], gate_ref[...], preferred_element_type=f32)
-        )
-        return carry
-
-    lax.fori_loop(0, rows // step_rows, gate_step, 0)
+        for u in range(4):
+            i = b * 4 + u
+            block = normed[pl.ds(pl.multiple_of(i * cols, 16), LANES), :]
+            gating[i] = jax.nn.sigmoid(
+                lax.dot_general(
+                    gate_ref[...], block, (((1,), (1,)), ((), ())), preferred_element_type=f32
+                )
+            )
+        return carry
+
+    lax.fori_loop(0, rows // 4, gate_step, 0)
     ow_pad[...] = jnp.zeros_like(ow_pad)
     stretch = ow_pad.shape[0] // 2
+    square = jnp.concatenate(
+        [out_weight_ref[...].astype(f32), jnp.zeros((LANES - half, channels), f32)], axis=0
+    )
+    turned = jnp.transpose(square)
     for cc in range(2):
-        ow_pad[cc * stretch : cc * stretch + half, 0:half] = out_weight_ref[
-            cc * half : (cc + 1) * half, :
-        ].astype(f32)
-    mix_w[...] = jnp.zeros_like(mix_w)
-    for rr in range(ratio):
-        for s in range(per):
-            for cc in range(2):
-                piece = ow_pad[pl.ds(cc * stretch + s, slot, stride=per), :]
-                at = rr * 2 * slot + cc * slot
-                mix_w[rr, s, at : at + slot, :] = piece.astype(bf16)
+        ow_pad[cc * stretch : cc * stretch + half, :] = turned[cc * half : (cc + 1) * half, :]
+    for s in range(per):
+        parts = [ow_pad[pl.ds(cc * stretch + s, slot, stride=per), :] for cc in range(2)]
+        parts.append(jnp.zeros((LANES - 2 * slot, LANES), f32))
+        back = jnp.transpose(jnp.concatenate(parts, axis=0))
+        mix_w[s * half : (s + 1) * half, :] = back[:half].astype(bf16)
     spread_t[...] = jnp.zeros_like(spread_t)
 
     def ring_step(d, carry):
@@ -278,7 +283,7 @@
 
         return carry
 
-    lax.fori_loop(1, nz, ring_step, 0)
+    lax.fori_loop(1, nz - 1, ring_step, 0)
 
     group_lane = lax.broadcasted_iota(jnp.int32, (1, LANES), 1)
 
@@ -311,7 +316,7 @@
             device_id_type=MESH,
         )
 
-    for sub in range(ratio):
+    def send_sub(sub):
         for c in range(chunks):
 
             def arrive(t, carry):
@@ -330,7 +335,6 @@
             lax.fori_loop(bounds[c], bounds[c + 1], finish, 0)
             c_copy(sub, c).start()
 
-    valid = lax.broadcasted_iota(jnp.int32, (2 * rows, LANES), 1) < 0
     row_at = lax.broadcasted_iota(jnp.int32, (2 * rows, LANES), 0) // rows
     lane_at = lax.broadcasted_iota(jnp.int32, (2 * rows, LANES), 1) // rows
     valid = (((pairs - 1) * 2 + row_at) * per + lane_at) < half
@@ -347,7 +351,7 @@
         result = result * (1.0 / channels)
         return jnp.concatenate([result, result], axis=0)
 
-    for sub in range(ratio):
+    def norm_sub(sub):
         for c in range(chunks):
             c_copy(sub, c).wait_recv()
 
@@ -386,29 +390,42 @@
 
         lax.fori_loop(0, pairs, normalise, 0)
 
-    batch = 8
+    order = jnp.where(2 * z >= nz, ratio - 1, 0)
+    step_sign = jnp.where(2 * z >= nz, -1, 1)
+    for t in range(ratio - 1):
+        send_sub(order + step_sign * t)
+    for t in range(ratio - 1):
+        norm_sub(order + step_sign * t)
+    ring_step(nz - 1, 0)
+    send_sub(order + step_sign * (ratio - 1))
+    norm_sub(order + step_sign * (ratio - 1))
+
+    wide = lax.broadcasted_iota(jnp.int32, (half, LANES), 1)
+
+    def mix_one(i):
+        start = pl.multiple_of(i * LANES, LANES)
+        tile = spread_t[pl.ds(start, LANES), :].astype(bf16)
+        parts = [tile[rr * 2 * slot : (rr + 1) * 2 * slot] for rr in range(ratio)]
+        res = jnp.dot(
+            mix_w[:, 0 : 2 * slot], jnp.concatenate(parts, axis=1), preferred_element_type=f32
+        )
+        mixing = None
+        for rr in range(ratio):
+            total = None
+            for s in range(per):
+                piece = res[s * half : (s + 1) * half, rr * LANES : (rr + 1) * LANES]
+                shift = (rr - s) * rows % LANES
+                piece = pltpu.roll(piece, shift, 1) if shift else piece
+                total = piece if total is None else total + piece
+            mixing = total if mixing is None else jnp.where(wide >= rr * rows, total, mixing)
+        out_ref[i] = (gating[i] * mixing)[:, :cols].astype(bf16)
 
     def mix_step(b, carry):
-        pieces = [[] for _ in range(per)]
-        for u in range(batch):
-            start = pl.multiple_of((b * batch + u) * LANES, LANES)
-            tile = jnp.transpose(spread_t[pl.ds(start, LANES), :])
-            for s in range(per):
-                pieces[s].append(tile[s * rows : (s + 1) * rows])
-        blocks = [jnp.concatenate(piece, axis=0).astype(bf16) for piece in pieces]
-        mixed = []
-        for rr in range(ratio):
-            total = jnp.dot(blocks[0], mix_w[rr, 0], preferred_element_type=f32)
-            for s in range(1, per):
-                total = total + jnp.dot(blocks[s], mix_w[rr, s], preferred_element_type=f32)
-            mixed.append(total[:, :half].reshape(batch, rows, half))
-        mixing = jnp.concatenate(mixed, axis=1)
-        start = pl.multiple_of(b * batch * cols, 16)
-        gates = gating[pl.ds(start, batch * cols), :].reshape(batch, cols, half)
-        out_ref[pl.ds(b * batch, batch)] = (gates * mixing).astype(bf16)
-        return carry
-
-    lax.fori_loop(0, rows // batch, mix_step, 0)
+        for u in range(4):
+            mix_one(b * 4 + u)
+        return carry
+
+    lax.fori_loop(0, rows // 4, mix_step, 0)
 
     others = peaks.at[pl.ds(0, members - 1)]
     pltpu.make_async_copy(others, others, peak_recv).wait()
@@ -477,7 +494,7 @@
     update, new_amax = pl.pallas_call(
         functools.partial(kernel, (nz, ny, rows, cols, half, chunks)),
         out_shape=(
-            jax.ShapeDtypeStruct((rows, cols, half), bf16),
+            jax.ShapeDtypeStruct((rows, half, cols), bf16),
             jax.ShapeDtypeStruct((2, half), f32),
         ),
         in_specs=[vmem, vmem, vmem, smem, vmem, vmem, vmem, vmem, smem, smem, vmem],
@@ -496,9 +513,9 @@
             pltpu.VMEM((ny, ratio, pairs) + tile, bf16),
             pltpu.VMEM((2, ratio, pairs) + tile, bf16),
             pltpu.VMEM((rows * LANES, LANES), f32),
-            pltpu.VMEM((ratio, per, LANES, LANES), bf16),
+            pltpu.VMEM((per * half, LANES), bf16),
             pltpu.VMEM((2 * slot * per, LANES), f32),
-            pltpu.VMEM((rows * cols, half), f32),
+            pltpu.VMEM((rows, half, LANES), f32),
             pltpu.VMEM((members, 8, channels), f32),
             dma,
             dma,
@@ -515,17 +532,17 @@
     )(
         pair_rep[0],
         pair_mask[0],
-        amax_history.reshape(1, channels),
+        amax_history,
         amax_history,
         in_gain.reshape(1, channels),
         in_bias.reshape(1, channels),
         weights,
-        gate_weight,
+        gate_weight.T,
         out_gain,
         out_bias,
-        out_weight,
+        out_weight.T,
     )
-    return update[None], new_amax
+    return jnp.transpose(update, (0, 2, 1))[None], new_amax
 
 
 def solution(mesh):

time: 56.6 us -> 53.1 us (0.938)
  the two profiles are of different devices: /device:TPU:25 before, /device:TPU:3 now
where the time goes in v2:
time: 53.1 us; the launch traced here: 52.9 us
  Pallas kernels  49.7 us (94%)
  local copies, waits for them, and re-layouts  2.53 us (5%)
  between operations  0.65 us (1%)
    pallas_call x1, Pallas kernels, on_device(): pl.pallas_call(functools.partial(kernel, (nz, ny, rows, cols, half, chunk...  49.7 us
    unnamed x4, local copies, waits for them, and re-layouts  2.53 us

profile of v2, /device:TPU:3, one launch (start us, length us, event | category | flops | bytes accessed | tf_op | source)
XLA Modules:
  0.0 52.9 jit_solution(2736983451841253226)
XLA Ops:
  0.6 49.7 %shard_map.113 = (bf16[40,64,80]{2,1,0:T(8,128)(2,1)}, f32[2,64]{1,0:T(2,128)}) custom-call(bf16[40,80,128]{2,1,0:T(8,128)(2,1)} %bitcast.12, s32[40,80]{1,0:T(8,128)} %bitcast.15, f32[2,64]{1,0:T(2,128)} %hist_smem.1, f32[2,64]{1,0:T(2,128)} %hist_smem.1, f32[1,128]{1,0:T(1,128)} %bitcast.18, f32[1,128]{1,0:T(1,128)} %bitcast.19, ...), custom_call_target="tpu_custom_call" | custom-call | tf_op jit(solution)/shard_map/pallas_call | solution.py:494
  50.4 0.0 copy-start
  50.4 2.0 %copy.14 = bf16[1,40,80,64]{2,3,1,0:T(8,128)(2,1)} copy(bf16[1,40,80,64]{2,3,1,0:T(8,128)(2,1)} %bitcast.13) | data formatting | bytes 819200
  52.4 0.0 copy-done
  52.4 0.6 %copy.15 = f32[2,64]{1,0:T(2,128)} copy(f32[2,64]{1,0:T(2,128)S(1)} %copy-done) | data formatting | bytes 1024
Async XLA Ops:
  50.4 2.0 %copy-start = (f32[2,64]{1,0:T(2,128)S(1)}, f32[2,64]{1,0:T(2,128)}, u32[]{:S(2)}) copy-start(f32[2,64]{1,0:T(2,128)} %get-tuple-element.9) | copy-start | bytes 1540

commit v3 on v2

--- a/solution.py
+++ b/solution.py
@@ -36,6 +36,10 @@
     left_s,
     right_s,
     left_b,
+    left_t,
+    left_e,
+    edge_t,
+    edge_in,
     right_all,
     own_t,
     send_t,
@@ -45,6 +49,9 @@
     mix_w,
     ow_pad,
     gating,
+    mixed,
+    out_v,
+    out_sem,
     peaks,
     peak_send,
     peak_recv,
@@ -54,6 +61,10 @@
     x_recv,
     c_send,
     c_recv,
+    left_send,
+    left_recv,
+    edge_send,
+    edge_recv,
 ):
     nz, ny, rows, cols, half, chunks = dims
     ratio = nz // ny
@@ -162,6 +173,43 @@
     for g in range(groups):
         left_b[g] = left_s[g * span : g * span + LANES, :].astype(bf16)
 
+    is_end = (z == 0) | (z == nz - 1)
+    is_next = (z == 1) | (z == nz - 2)
+    upper = 2 * z >= nz
+    inward = jnp.where(upper, z - 1, z + 1)
+    outward = jnp.where(upper, z + 1, z - 1)
+    far = jnp.where(upper, 0, nz - 1)
+
+    def left_copy(c):
+        window = pl.ds(2 * bounds[c], 2 * (bounds[c + 1] - bounds[c]))
+        return pltpu.make_async_remote_copy(
+            src_ref=left_t.at[window],
+            dst_ref=left_e.at[window],
+            send_sem=left_send.at[c],
+            recv_sem=left_recv.at[c],
+            device_id={"gx": inward},
+            device_id_type=MESH,
+        )
+
+    def edge_copy(c):
+        window = pl.ds(bounds[c], bounds[c + 1] - bounds[c])
+        return pltpu.make_async_remote_copy(
+            src_ref=edge_t.at[window],
+            dst_ref=edge_in.at[window],
+            send_sem=edge_send.at[c],
+            recv_sem=edge_recv.at[c],
+            device_id={"gx": outward},
+            device_id_type=MESH,
+        )
+
+    @pl.when(is_end)
+    def _():
+        for c in range(chunks):
+            for g in range(2 * bounds[c], 2 * bounds[c + 1]):
+                tile = jnp.transpose(left_s[g * span : g * span + LANES, :])
+                left_t[g] = tile[:cols].astype(bf16)
+            left_copy(c).start()
+
     peaks[me] = jnp.broadcast_to(jnp.max(jnp.transpose(peak[...]), axis=0, keepdims=True), (8, channels))
 
     def spread_peak(t, carry):
@@ -180,11 +228,15 @@
 
     lane = lax.broadcasted_iota(jnp.int32, (rows, LANES), 1)
 
-    def triangle_pair(r, p):
+    def triangle_pair(r, p, edge=False):
         halves = []
         for u in range(2):
+            if edge:
+                tile = jnp.transpose(left_e[2 * p + u].astype(f32)).astype(bf16)
+            else:
+                tile = left_b[2 * p + u][:, :cols]
             res = lax.dot_general(
-                left_b[2 * p + u][:, :cols],
+                tile,
                 right_all[r, 2 * p + u],
                 (((1,), (0,)), ((), ())),
                 preferred_element_type=f32,
@@ -261,7 +313,7 @@
             def _():
                 z_copy(low, c, 0).wait_recv()
 
-                @pl.when(z < nz - 1)
+                @pl.when((z < nz - 1) & ((z < nz - 2) | (low > 0)))
                 def _():
                     z_copy(low, c, 0).start()
 
@@ -269,7 +321,7 @@
             def _():
                 z_copy(high, c, 1).wait_recv()
 
-                @pl.when(z > 0)
+                @pl.when((z > 0) & ((z > 1) | (high < nz - 1)))
                 def _():
                     z_copy(high, c, 1).start()
 
@@ -281,7 +333,35 @@
             def _():
                 triangle_block(high, c)
 
-        return carry
+            @pl.when((d == nz - 2) & is_next)
+            def _():
+                left_copy(c).wait_recv()
+                for p in range(bounds[c], bounds[c + 1]):
+                    edge_t[p] = triangle_pair(far, p, True).astype(bf16)
+                edge_copy(c).start()
+
+        return carry
+
+    def edge_step():
+        owner, sub = far // ratio, lax.rem(far, ratio)
+        for c in range(chunks):
+            window = pl.ds(bounds[c], bounds[c + 1] - bounds[c])
+            edge_copy(c).wait_recv()
+
+            @pl.when(owner == y)
+            def _():
+                own_t[sub, window] = edge_in[window].astype(f32)
+
+            @pl.when(owner != y)
+            def _():
+                pltpu.make_async_remote_copy(
+                    src_ref=edge_in.at[window],
+                    dst_ref=recv_t.at[y, sub, window],
+                    send_sem=x_send.at[owner, sub, c],
+                    recv_sem=x_recv.at[y, sub, c],
+                    device_id={"gy": owner},
+                    device_id_type=MESH,
+                ).start()
 
     lax.fori_loop(1, nz - 1, ring_step, 0)
 
@@ -390,42 +470,57 @@
 
         lax.fori_loop(0, pairs, normalise, 0)
 
+    wide = lax.broadcasted_iota(jnp.int32, (half, LANES), 1)
+
+    def mix_sub(sub, last):
+        def two_rows(i):
+            parts = []
+            for u in range(2):
+                start = pl.multiple_of((i + u) * LANES + sub * (2 * slot), 2 * slot)
+                parts.append(spread_t[pl.ds(start, 2 * slot), :].astype(bf16))
+            res = jnp.dot(
+                mix_w[:, 0 : 2 * slot], jnp.concatenate(parts, axis=1), preferred_element_type=f32
+            )
+            for u in range(2):
+                total = res[:half, u * LANES : (u + 1) * LANES]
+                for s in range(1, per):
+                    piece = res[s * half : (s + 1) * half, u * LANES : (u + 1) * LANES]
+                    total = total + pltpu.roll(piece, LANES - s * rows, 1)
+                mixed[sub, i + u] = total
+
+        def out_row(i):
+            mixing = mixed[0, i]
+            for rr in range(1, ratio):
+                moved = pltpu.roll(mixed[rr, i], rr * rows, 1)
+                mixing = jnp.where(wide >= rr * rows, moved, mixing)
+            out_v[i] = (gating[i] * mixing)[:, :cols].astype(bf16)
+
+        def mix_step(b, carry):
+            for u in range(2):
+                two_rows(b * 4 + 2 * u)
+            if last:
+                for u in range(4):
+                    out_row(b * 4 + u)
+                out_copy(b).start()
+            return carry
+
+        lax.fori_loop(0, rows // 4, mix_step, 0)
+
+    def out_copy(b):
+        window = pl.ds(b * 4, 4)
+        return pltpu.make_async_copy(out_v.at[window], out_ref.at[window], out_sem.at[b])
+
     order = jnp.where(2 * z >= nz, ratio - 1, 0)
     step_sign = jnp.where(2 * z >= nz, -1, 1)
     for t in range(ratio - 1):
         send_sub(order + step_sign * t)
     for t in range(ratio - 1):
         norm_sub(order + step_sign * t)
-    ring_step(nz - 1, 0)
+        mix_sub(order + step_sign * t, False)
+    pl.when(is_end)(edge_step)
     send_sub(order + step_sign * (ratio - 1))
     norm_sub(order + step_sign * (ratio - 1))
-
-    wide = lax.broadcasted_iota(jnp.int32, (half, LANES), 1)
-
-    def mix_one(i):
-        start = pl.multiple_of(i * LANES, LANES)
-        tile = spread_t[pl.ds(start, LANES), :].astype(bf16)
-        parts = [tile[rr * 2 * slot : (rr + 1) * 2 * slot] for rr in range(ratio)]
-        res = jnp.dot(
-            mix_w[:, 0 : 2 * slot], jnp.concatenate(parts, axis=1), preferred_element_type=f32
-        )
-        mixing = None
-        for rr in range(ratio):
-            total = None
-            for s in range(per):
-                piece = res[s * half : (s + 1) * half, rr * LANES : (rr + 1) * LANES]
-                shift = (rr - s) * rows % LANES
-                piece = pltpu.roll(piece, shift, 1) if shift else piece
-                total = piece if total is None else total + piece
-            mixing = total if mixing is None else jnp.where(wide >= rr * rows, total, mixing)
-        out_ref[i] = (gating[i] * mixing)[:, :cols].astype(bf16)
-
-    def mix_step(b, carry):
-        for u in range(4):
-            mix_one(b * 4 + u)
-        return carry
-
-    lax.fori_loop(0, rows // 4, mix_step, 0)
+    mix_sub(order + step_sign * (ratio - 1), True)
 
     others = peaks.at[pl.ds(0, members - 1)]
     pltpu.make_async_copy(others, others, peak_recv).wait()
@@ -433,6 +528,12 @@
     amax_ref[0:1, :] = top[:, :half]
     amax_ref[1:2, :] = top[:, half:]
 
+    def drain_out(b, carry):
+        out_copy(b).wait()
+        return carry
+
+    lax.fori_loop(0, rows // 4, drain_out, 0)
+
     pltpu.make_async_copy(others, others, peak_send).wait()
     for sub in range(ratio):
         for c in range(chunks):
@@ -449,17 +550,27 @@
     def drain_z(source, carry):
         for c in range(chunks):
 
-            @pl.when((source <= z) & (z < nz - 1))
+            @pl.when((source <= z) & (z < nz - 1) & ((z < nz - 2) | (source > 0)))
             def _():
                 z_copy(source, c, 0).wait_send()
 
-            @pl.when((source >= z) & (z > 0))
+            @pl.when((source >= z) & (z > 0) & ((z > 1) | (source < nz - 1)))
             def _():
                 z_copy(source, c, 1).wait_send()
 
         return carry
 
     lax.fori_loop(0, nz, drain_z, 0)
+
+    @pl.when(is_end)
+    def _():
+        for c in range(chunks):
+            left_copy(c).wait_send()
+
+    @pl.when(is_next)
+    def _():
+        for c in range(chunks):
+            edge_copy(c).wait_send()
 
 
 def on_device(
@@ -478,7 +589,7 @@
 ):
     crops, rows, cols, channels = pair_rep.shape
     half = proj_weight.shape[2]
-    chunks = 2
+    chunks = 4
     ratio = nz // ny
     per = LANES // rows
     pairs = -(-half // (2 * per))
@@ -498,7 +609,7 @@
             jax.ShapeDtypeStruct((2, half), f32),
         ),
         in_specs=[vmem, vmem, vmem, smem, vmem, vmem, vmem, vmem, smem, smem, vmem],
-        out_specs=(vmem, vmem),
+        out_specs=(pl.BlockSpec(memory_space=pl.ANY), vmem),
         scratch_shapes=[
             pltpu.VMEM((rows * cols + LANES, channels), bf16),
             pltpu.VMEM((rows, LANES), f32),
@@ -507,6 +618,10 @@
             pltpu.VMEM((scratch_rows, LANES), f32),
             pltpu.VMEM((scratch_rows, LANES), f32),
             pltpu.VMEM((groups, LANES, LANES), bf16),
+            pltpu.VMEM((groups, cols, LANES), bf16),
+            pltpu.VMEM((groups, cols, LANES), bf16),
+            pltpu.VMEM((pairs,) + tile, bf16),
+            pltpu.VMEM((pairs,) + tile, bf16),
             pltpu.VMEM((nz, groups, cols, LANES), bf16),
             pltpu.VMEM((ratio, pairs) + tile, f32),
             pltpu.VMEM((ny, ratio, pairs) + tile, bf16),
@@ -516,6 +631,9 @@
             pltpu.VMEM((per * half, LANES), bf16),
             pltpu.VMEM((2 * slot * per, LANES), f32),
             pltpu.VMEM((rows, half, LANES), f32),
+            pltpu.VMEM((ratio, rows, half, LANES), f32),
+            pltpu.VMEM((rows, half, cols), bf16),
+            dma((rows // 4,)),
             pltpu.VMEM((members, 8, channels), f32),
             dma,
             dma,
@@ -525,6 +643,10 @@
             dma((ny, ratio, chunks)),
             dma((ratio, chunks)),
             dma((ratio, chunks)),
+            dma((chunks,)),
+            dma((chunks,)),
+            dma((chunks,)),
+            dma((chunks,)),
         ],
         compiler_params=pltpu.CompilerParams(
             collective_id=0, has_side_effects=True, vmem_limit_bytes=56 * 1024 * 1024

time: 53.1 us -> 53.2 us (level)
  no operation moved by 1% of the time
where the time goes in v3:
time: 53.2 us; the launch traced here: 53.1 us
  Pallas kernels  49.9 us (94%)
  local copies, waits for them, and re-layouts  2.53 us (5%)
  between operations  0.65 us (1%)
    pallas_call x1, Pallas kernels, on_device(): pl.pallas_call(functools.partial(kernel, (nz, ny, rows, cols, half, chunk...  49.9 us
    unnamed x4, local copies, waits for them, and re-layouts  2.53 us

profile of v3, /device:TPU:3, one launch (start us, length us, event | category | flops | bytes accessed | tf_op | source)
XLA Modules:
  0.0 53.1 jit_solution(13622374623619483234)
XLA Ops:
  0.6 49.9 %shard_map.113 = (bf16[40,64,80]{2,1,0:T(8,128)(2,1)}, f32[2,64]{1,0:T(2,128)}) custom-call(bf16[40,80,128]{2,1,0:T(8,128)(2,1)} %bitcast.12, s32[40,80]{1,0:T(8,128)} %bitcast.15, f32[2,64]{1,0:T(2,128)} %hist_smem.1, f32[2,64]{1,0:T(2,128)} %hist_smem.1, f32[1,128]{1,0:T(1,128)} %bitcast.18, f32[1,128]{1,0:T(1,128)} %bitcast.19, ...), custom_call_target="tpu_custom_call" | custom-call | tf_op jit(solution)/shard_map/pallas_call | solution.py:605
  50.5 0.0 copy-start
  50.5 2.0 %copy.14 = bf16[1,40,80,64]{2,3,1,0:T(8,128)(2,1)} copy(bf16[1,40,80,64]{2,3,1,0:T(8,128)(2,1)} %bitcast.13) | data formatting | bytes 819200
  52.5 0.0 copy-done
  52.5 0.6 %copy.15 = f32[2,64]{1,0:T(2,128)} copy(f32[2,64]{1,0:T(2,128)S(1)} %copy-done) | data formatting | bytes 1024
Async XLA Ops:
  50.5 2.0 %copy-start = (f32[2,64]{1,0:T(2,128)S(1)}, f32[2,64]{1,0:T(2,128)}, u32[]{:S(2)}) copy-start(f32[2,64]{1,0:T(2,128)} %get-tuple-element.9) | copy-start | bytes 1540
